TPU v7x, 512 devices: a 4x2x32 block of a 4x8x32 slice. The times are simulated.
512 devices in a mesh: groups: 2 (over y), rows: 32 (over z), keys: 4 (over x), heads: 2 (over core).
Axes of the slice: x: 4, y: 2, z: 32, core: 2. Of those that a mesh axis runs over, the one named last changes fastest.
The devices are a block of a 4x8x32 slice.
Arguments:
- pair: bfloat16 [2048, 1024, 128], P(('groups', 'rows'), 'keys'), parts along dimension 0, may hold values from -6 to 6
- seq_length: int32 [2], P('groups'), parts along dimension 0, may hold values from 513 to 1024
- tile_counts: int32 [2048, 8], P(('groups', 'rows')), parts along dimension 0, may hold values from 0 to 128, as said below
- ln_gain: float32 [128], replicated, may hold values from 0.5 to 1.5
- w_query: bfloat16 [128, 128], P(None, 'heads'), may hold values from -8 to 8
- w_key: bfloat16 [128, 128], P(None, 'heads'), may hold values from -0.5 to 0.5
- w_value: bfloat16 [128, 128], P(None, 'heads'), may hold values from -0.5 to 0.5
- w_gate: bfloat16 [128, 128], P(None, 'heads'), may hold values from -0.5 to 0.5
- w_bias: bfloat16 [128, 4], P(None, 'heads'), may hold values from -1.5 to 1.5
- w_out: bfloat16 [128, 128], replicated, may hold values from -2 to 2
Outputs:
- update: bfloat16 [2048, 1024, 128], P(('groups', 'rows'), ('keys', 'heads')), parts along dimension 0
There are 2 independent parts, one for each index of `groups`. A program takes and returns all parts, laid end to end along the dimension named above; an argument that names none is the same for every part. Nothing has to cross between parts.
Inputs may be any that keep to these rules, and one draw needn't show every extreme that they name: `tile_counts`: for each row and each tile of 128 keys, how many of the tile's leading keys are valid; some rows have no valid key at all.
All inputs are finite; a program needn't handle non-finite values.
Results may differ from a plain program's by a relative error of at most 0.03.
The roundings to bfloat16 on the way count: a program that leaves them out, or rounds other values in their place, can miss the bound.
Values may be sent and summed in bfloat16 or wider, within the bound.
A program may use at most 128 MiB of HBM per device.

v0:
```python
import jax
import jax.numpy as jnp
from jax import lax
from jax.sharding import PartitionSpec as P

HEAD_DIM = 32
TILE = 128
norm_epsilon = 1e-05
masked_score = -1e30


def from_everyone(value, axis):
    peers = lax.axis_size(axis)
    return lax.all_to_all(
        jnp.broadcast_to(value[None], (peers, *value.shape)), axis, 0, 0, tiled=True
    )


def laid_out(tiles, dim):
    tiles = jnp.moveaxis(tiles, 0, dim)
    dims = tiles.shape
    return tiles.reshape(*dims[:dim], dims[dim] * dims[dim + 1], *dims[dim + 2 :])


def gathered_copies(value, axis, dim):
    tiles = from_everyone(value, axis)
    return laid_out(tiles, dim)


def sent_together(arrays, axis, dim, along):
    ends, at = ([], 0)
    for a in arrays[:-1]:
        at += a.shape[along]
        ends.append(at)
    both = jnp.concatenate(arrays, axis=along)
    return tuple(jnp.split(lax.all_gather(both, axis, axis=dim, tiled=True), ends, axis=along))


def exchange_in_groups(value, axis, split_dim, concat_dim, work, item_dim, out_dim):
    items = jax.tree.leaves(value)[0].shape[item_dim]
    count = 2 if items % 2 == 0 else 1
    done = []
    for k in range(count):
        group = jax.tree.map(
            lambda a: lax.slice_in_dim(
                a, k * (items // count), (k + 1) * (items // count), axis=item_dim
            ),
            value,
        )
        done.append(
            work(
                lax.all_to_all(
                    group, axis, split_axis=split_dim, concat_axis=concat_dim, tiled=True
                )
            )
        )
    return jax.tree.map(lambda *parts: jnp.concatenate(parts, axis=out_dim), *done)


def layer_norm(values, gain):
    center = values - jnp.mean(values, axis=-1, keepdims=True)
    spread = jnp.mean(center * center, axis=-1, keepdims=True)
    return center * lax.rsqrt(spread + norm_epsilon) * gain


def finish(row_sum, weighted):
    denom = jnp.maximum(row_sum, 1.0)
    result = weighted / denom[..., None]
    rows_dev, heads_dev, cols_dev, depth = result.shape
    result = jnp.transpose(result, (0, 2, 1, 3)).reshape(rows_dev, cols_dev, heads_dev * depth)
    return result.astype(jnp.bfloat16)


def per_device(
    pair, seq_length, tile_counts, ln_gain, w_query, w_key, w_value, w_gate, w_bias, w_out
):
    rows_dev, cols_dev, channels = pair.shape
    key_groups = lax.axis_size("keys")
    length_all = cols_dev * key_groups
    heads_dev = w_bias.shape[1]
    width_dev = heads_dev * HEAD_DIM
    normed = layer_norm(pair.astype(jnp.float32), ln_gain).astype(jnp.bfloat16)
    flat = normed.reshape(rows_dev * cols_dev, channels)
    queries = (
        (jnp.dot(flat, w_query, preferred_element_type=jnp.float32) * HEAD_DIM ** (-0.5))
        .astype(jnp.bfloat16)
        .reshape(rows_dev, cols_dev, heads_dev, HEAD_DIM)
    )
    keys_local = (
        jnp.dot(flat, w_key, preferred_element_type=jnp.float32)
        .astype(jnp.bfloat16)
        .reshape(rows_dev, cols_dev, heads_dev, HEAD_DIM)
    )
    values_local = (
        jnp.dot(flat, w_value, preferred_element_type=jnp.float32)
        .astype(jnp.bfloat16)
        .reshape(rows_dev, cols_dev, heads_dev, HEAD_DIM)
    )
    gate_act = jax.nn.sigmoid(jnp.dot(flat, w_gate, preferred_element_type=jnp.float32)).reshape(
        rows_dev, cols_dev, width_dev
    )
    bias_local = jnp.einsum("rkc,ch->hrk", normed, w_bias, preferred_element_type=jnp.float32)
    bias_rows = gathered_copies(bias_local.astype(jnp.bfloat16), "rows", 1).astype(bias_local.dtype)
    positions = jnp.arange(length_all, dtype=jnp.int32)
    allowed = (positions[None, :] < seq_length[0]) & (
        (positions % TILE)[None, :] < jnp.repeat(tile_counts, TILE, axis=1)
    )
    bias_turn = lax.all_to_all(
        bias_rows.astype(jnp.bfloat16), "keys", split_axis=1, concat_axis=2, tiled=True
    ).astype(bias_rows.dtype)
    initial = (
        jnp.full((rows_dev, heads_dev, cols_dev), masked_score, jnp.float32),
        jnp.zeros((rows_dev, heads_dev, cols_dev), jnp.float32),
        jnp.zeros((rows_dev, heads_dev, cols_dev, HEAD_DIM), jnp.float32),
    )
    piece_keys, piece_values = sent_together((keys_local, values_local), "keys", 1, 0)

    def one_tile(tile_index, state):
        row_max, row_sum, weighted = state
        offset = tile_index * TILE
        key_tile = lax.dynamic_slice_in_dim(piece_keys, offset, TILE, 1)
        value_tile = lax.dynamic_slice_in_dim(piece_values, offset, TILE, 1)
        tile_bias = lax.dynamic_slice_in_dim(bias_turn, offset, TILE, 2)
        shown = lax.dynamic_slice_in_dim(allowed, offset, TILE, 1)[:, None, None, :]
        scores = (
            jnp.einsum("rjhd,rkhd->rhjk", queries, key_tile, preferred_element_type=jnp.float32)
            + tile_bias[None]
        )
        scores = jnp.where(shown, scores, masked_score)
        new_max = jnp.maximum(row_max, jnp.max(scores, axis=-1))
        weights = jnp.where(shown, jnp.exp(scores - new_max[..., None]), 0.0)
        rescale = jnp.exp(row_max - new_max)
        row_sum = row_sum * rescale + jnp.sum(weights, axis=-1)
        weighted = weighted * rescale[..., None] + jnp.einsum(
            "rhjk,rkhd->rhjd",
            weights.astype(jnp.bfloat16),
            value_tile,
            preferred_element_type=jnp.float32,
        )
        return (new_max, row_sum, weighted)

    row_max, row_sum, weighted = lax.fori_loop(0, piece_keys.shape[1] // TILE, one_tile, initial)
    attended = finish(row_sum, weighted)
    attended = lax.optimization_barrier(attended).astype(jnp.float32)
    gated = (gate_act * attended).astype(jnp.bfloat16)

    def project(mixed):
        return jnp.einsum("rkc,cd->rkd", mixed, w_out, preferred_element_type=jnp.float32).astype(
            jnp.bfloat16
        )

    return exchange_in_groups(gated, "heads", 1, 2, project, 0, 0)


def solution(mesh):
    in_specs = (
        P(("groups", "rows"), "keys", None),
        P("groups"),
        P(("groups", "rows"), None),
        P(),
        P(None, "heads"),
        P(None, "heads"),
        P(None, "heads"),
        P(None, "heads"),
        P(None, "heads"),
        P(),
    )
    out_specs = P(("groups", "rows"), ("keys", "heads"), None)
    return jax.shard_map(
        per_device, mesh=mesh, in_specs=in_specs, out_specs=out_specs, check_vma=False
    )
```

profile of v0, /device:TPU:33, one launch (start us, length us, event | category | flops | bytes accessed | tf_op | source)
XLA Modules:
  0.0 321.6 jit_solution(10131734697609890808)
XLA Ops:
  6.6 2.4 convert_reduce_fusion
  9.0 2.4 fusion.25
  11.4 2.5 fusion.27
  13.9 0.8 convolution_convert_fusion
  15.6 0.8 convolution_convert_fusion.1
  17.3 1.5 pad_maximum_fusion
  19.5 0.6 fusion.29
  20.2 1.1 broadcast_in_dim.74
  21.3 46.3 %all-to-all-start = ((bf16[32,2,32,256]{3,2,1,0:T(8,128)(2,1)}), bf16[32,2,32,256]{3,2,1,0:T(8,128)(2,1)}, u32[]{:S(2)}, u32[]{:S(2)}) async-start(bf16[32,2,32,256]{3,2,1,0:T(8,128)(2,1)} %broadcast_in_dim.74), calls=%async_computation | async-start | bytes 2097152 | tf_op jit(solution)/shard_map/all_to_all | solution.py:14
  68.3 0.8 fusion.22
  69.1 103.0 %all-to-all-done = bf16[32,2,32,256]{3,2,1,0:T(8,128)(2,1)} async-done(((bf16[32,2,32,256]{3,2,1,0:T(8,128)(2,1)}), bf16[32,2,32,256]{3,2,1,0:T(8,128)(2,1)}, u32[]{:S(2)}, u32[]{:S(2)}) %all-to-all-start) | async-done | bytes 1048608 | tf_op jit(solution)/shard_map/all_to_all | solution.py:14
  172.1 1.3 copy.64
  173.4 2.0 copy.65
  175.5 4.5 %all-to-all-start.1 = ((bf16[2,1024,256]{2,0,1:T(2,128)(2,1)}), bf16[2,1024,256]{2,0,1:T(2,128)(2,1)}, u32[]{:S(2)}, u32[]{:S(2)}) async-start(bf16[2,1024,256]{2,0,1:T(2,128)(2,1)} %copy.65), calls=%async_computation.1 | async-start | bytes 2097152 | tf_op jit(solution)/shard_map/all_to_all | solution.py:108
  181.1 2.2 fusion.21
  183.4 10.9 %all-to-all-done.1 = bf16[2,1024,256]{2,0,1:T(2,128)(2,1)} async-done(((bf16[2,1024,256]{2,0,1:T(2,128)(2,1)}), bf16[2,1024,256]{2,0,1:T(2,128)(2,1)}, u32[]{:S(2)}, u32[]{:S(2)}) %all-to-all-start.1) | async-done | bytes 1048608 | tf_op jit(solution)/shard_map/all_to_all | solution.py:108
  194.2 1.4 copy.66
  195.8 1.8 copy.67
  197.7 6.4 %fusion.37 = (bf16[32,1024,2,32]{1,3,2,0:T(8,128)(2,1)}, bf16[32,1024,2,32]{1,3,2,0:T(8,128)(2,1)}) fusion(bf16[64,1024,2,32]{1,3,2,0:T(8,128)(2,1)} %all-gather.2.cloned.1.call-done), kind=kLoop, calls=%fused_computation.63 | loop fusion | bytes 16777216 | tf_op jit(solution)/shard_map/split | solution.py:36
  204.0 90.0 %while.18 = (s32[]{:T(128)}, f32[32,2,256]{2,1,0:T(2,128)S(1)}, f32[32,2,256]{2,1,0:T(2,128)S(1)}, f32[32,2,256,32]{2,3,1,0:T(8,128)S(1)}, pred[32,1024]{1,0:T(8...) while((s32[]{:T(128)}, f32[32,2,256]{2,1,0:T(2,128)S(1)}, ...), condition=%wide.region_5.6_spmd.clone, body=%wide.region_2.5_spmd.clone.sunk | while | flops 297353216 | bytes 33837260 | solution.py:142
  204.1 1.0 constant_dynamic-slice_fusion.4
  205.0 3.4 %fusion.62 = (f32[32,2,256]{2,1,0:T(2,128)S(1)}, f32[32,2,128,256]{3,2,1,0:T(8,128)S(1)}) fusion(f32[2,256,128]{1,2,0:T(8,128)S(1)} %constant_dynamic-slice_fusion.4, pred[32,128]{1,0:T(8,128)(4,1)S(1)} %constant_dynamic-slice_fusion.5, bf16[32,256,2,32]{1,3,2,0:T(8,128)(2,1)S(1)} %get-tuple-element.358, ...), kind=kOutput, calls=%fused_computation.3.clone.1 | convolution fusion | flops 140492800 | bytes 10293252 | tf_op jit(solution)/shard_map/while/body/eval_jaxpr/rjhd,rkhd->rhjk/dot_general | solution.py:126
  208.5 3.0 fusion.64
  211.6 3.6 %fusion.66 = f32[32,2,256,32]{2,3,1,0:T(8,128)S(1)} fusion(f32[32,2,256,32]{2,3,1,0:T(8,128)S(1)} %get-tuple-element.342, f32[32,2,128,256]{3,2,1,0:T(8,128)S(1)} %get-tuple-element.323, f32[32,2,256]{2,1,0:T(2,128)S(1)} %fusion.63, f32[2,256,128]{1,2,0:T(8,128)S(1)} %constant_dynamic-slice_fusion.4, ...), kind=kOutput, calls=%fused_computation.9.clone.1 | convolution fusion | flops 146276352 | bytes 13504517 | tf_op jit(solution)/shard_map/while/body/eval_jaxpr/rhjk,rkhd->rhjd/dot_general | solution.py:134
  215.3 1.0 constant_dynamic-slice_fusion.4
  216.3 3.4 %fusion.62 = (f32[32,2,256]{2,1,0:T(2,128)S(1)}, f32[32,2,128,256]{3,2,1,0:T(8,128)S(1)}) fusion(f32[2,256,128]{1,2,0:T(8,128)S(1)} %constant_dynamic-slice_fusion.4, pred[32,128]{1,0:T(8,128)(4,1)S(1)} %constant_dynamic-slice_fusion.5, bf16[32,256,2,32]{1,3,2,0:T(8,128)(2,1)S(1)} %get-tuple-element.358, ...), kind=kOutput, calls=%fused_computation.3.clone.1 | convolution fusion | flops 140492800 | bytes 10293252 | tf_op jit(solution)/shard_map/while/body/eval_jaxpr/rjhd,rkhd->rhjk/dot_general | solution.py:126
  219.7 3.0 fusion.64
  222.9 3.6 %fusion.66 = f32[32,2,256,32]{2,3,1,0:T(8,128)S(1)} fusion(f32[32,2,256,32]{2,3,1,0:T(8,128)S(1)} %get-tuple-element.342, f32[32,2,128,256]{3,2,1,0:T(8,128)S(1)} %get-tuple-element.323, f32[32,2,256]{2,1,0:T(2,128)S(1)} %fusion.63, f32[2,256,128]{1,2,0:T(8,128)S(1)} %constant_dynamic-slice_fusion.4, ...), kind=kOutput, calls=%fused_computation.9.clone.1 | convolution fusion | flops 146276352 | bytes 13504517 | tf_op jit(solution)/shard_map/while/body/eval_jaxpr/rhjk,rkhd->rhjd/dot_general | solution.py:134
  226.6 1.0 constant_dynamic-slice_fusion.4
  227.5 3.4 %fusion.62 = (f32[32,2,256]{2,1,0:T(2,128)S(1)}, f32[32,2,128,256]{3,2,1,0:T(8,128)S(1)}) fusion(f32[2,256,128]{1,2,0:T(8,128)S(1)} %constant_dynamic-slice_fusion.4, pred[32,128]{1,0:T(8,128)(4,1)S(1)} %constant_dynamic-slice_fusion.5, bf16[32,256,2,32]{1,3,2,0:T(8,128)(2,1)S(1)} %get-tuple-element.358, ...), kind=kOutput, calls=%fused_computation.3.clone.1 | convolution fusion | flops 140492800 | bytes 10293252 | tf_op jit(solution)/shard_map/while/body/eval_jaxpr/rjhd,rkhd->rhjk/dot_general | solution.py:126
  231.0 3.0 fusion.64
  234.1 3.6 %fusion.66 = f32[32,2,256,32]{2,3,1,0:T(8,128)S(1)} fusion(f32[32,2,256,32]{2,3,1,0:T(8,128)S(1)} %get-tuple-element.342, f32[32,2,128,256]{3,2,1,0:T(8,128)S(1)} %get-tuple-element.323, f32[32,2,256]{2,1,0:T(2,128)S(1)} %fusion.63, f32[2,256,128]{1,2,0:T(8,128)S(1)} %constant_dynamic-slice_fusion.4, ...), kind=kOutput, calls=%fused_computation.9.clone.1 | convolution fusion | flops 146276352 | bytes 13504517 | tf_op jit(solution)/shard_map/while/body/eval_jaxpr/rhjk,rkhd->rhjd/dot_general | solution.py:134
  237.8 1.0 constant_dynamic-slice_fusion.4
  238.8 3.4 %fusion.62 = (f32[32,2,256]{2,1,0:T(2,128)S(1)}, f32[32,2,128,256]{3,2,1,0:T(8,128)S(1)}) fusion(f32[2,256,128]{1,2,0:T(8,128)S(1)} %constant_dynamic-slice_fusion.4, pred[32,128]{1,0:T(8,128)(4,1)S(1)} %constant_dynamic-slice_fusion.5, bf16[32,256,2,32]{1,3,2,0:T(8,128)(2,1)S(1)} %get-tuple-element.358, ...), kind=kOutput, calls=%fused_computation.3.clone.1 | convolution fusion | flops 140492800 | bytes 10293252 | tf_op jit(solution)/shard_map/while/body/eval_jaxpr/rjhd,rkhd->rhjk/dot_general | solution.py:126
  242.2 3.0 fusion.64
  245.4 3.6 %fusion.66 = f32[32,2,256,32]{2,3,1,0:T(8,128)S(1)} fusion(f32[32,2,256,32]{2,3,1,0:T(8,128)S(1)} %get-tuple-element.342, f32[32,2,128,256]{3,2,1,0:T(8,128)S(1)} %get-tuple-element.323, f32[32,2,256]{2,1,0:T(2,128)S(1)} %fusion.63, f32[2,256,128]{1,2,0:T(8,128)S(1)} %constant_dynamic-slice_fusion.4, ...), kind=kOutput, calls=%fused_computation.9.clone.1 | convolution fusion | flops 146276352 | bytes 13504517 | tf_op jit(solution)/shard_map/while/body/eval_jaxpr/rhjk,rkhd->rhjd/dot_general | solution.py:134
  249.1 1.0 constant_dynamic-slice_fusion.4
  250.0 3.4 %fusion.62 = (f32[32,2,256]{2,1,0:T(2,128)S(1)}, f32[32,2,128,256]{3,2,1,0:T(8,128)S(1)}) fusion(f32[2,256,128]{1,2,0:T(8,128)S(1)} %constant_dynamic-slice_fusion.4, pred[32,128]{1,0:T(8,128)(4,1)S(1)} %constant_dynamic-slice_fusion.5, bf16[32,256,2,32]{1,3,2,0:T(8,128)(2,1)S(1)} %get-tuple-element.358, ...), kind=kOutput, calls=%fused_computation.3.clone.1 | convolution fusion | flops 140492800 | bytes 10293252 | tf_op jit(solution)/shard_map/while/body/eval_jaxpr/rjhd,rkhd->rhjk/dot_general | solution.py:126
  253.5 3.0 fusion.64
  256.6 3.6 %fusion.66 = f32[32,2,256,32]{2,3,1,0:T(8,128)S(1)} fusion(f32[32,2,256,32]{2,3,1,0:T(8,128)S(1)} %get-tuple-element.342, f32[32,2,128,256]{3,2,1,0:T(8,128)S(1)} %get-tuple-element.323, f32[32,2,256]{2,1,0:T(2,128)S(1)} %fusion.63, f32[2,256,128]{1,2,0:T(8,128)S(1)} %constant_dynamic-slice_fusion.4, ...), kind=kOutput, calls=%fused_computation.9.clone.1 | convolution fusion | flops 146276352 | bytes 13504517 | tf_op jit(solution)/shard_map/while/body/eval_jaxpr/rhjk,rkhd->rhjd/dot_general | solution.py:134
  260.3 1.0 constant_dynamic-slice_fusion.4
  261.3 3.4 %fusion.62 = (f32[32,2,256]{2,1,0:T(2,128)S(1)}, f32[32,2,128,256]{3,2,1,0:T(8,128)S(1)}) fusion(f32[2,256,128]{1,2,0:T(8,128)S(1)} %constant_dynamic-slice_fusion.4, pred[32,128]{1,0:T(8,128)(4,1)S(1)} %constant_dynamic-slice_fusion.5, bf16[32,256,2,32]{1,3,2,0:T(8,128)(2,1)S(1)} %get-tuple-element.358, ...), kind=kOutput, calls=%fused_computation.3.clone.1 | convolution fusion | flops 140492800 | bytes 10293252 | tf_op jit(solution)/shard_map/while/body/eval_jaxpr/rjhd,rkhd->rhjk/dot_general | solution.py:126
  264.7 3.0 fusion.64
  267.9 3.6 %fusion.66 = f32[32,2,256,32]{2,3,1,0:T(8,128)S(1)} fusion(f32[32,2,256,32]{2,3,1,0:T(8,128)S(1)} %get-tuple-element.342, f32[32,2,128,256]{3,2,1,0:T(8,128)S(1)} %get-tuple-element.323, f32[32,2,256]{2,1,0:T(2,128)S(1)} %fusion.63, f32[2,256,128]{1,2,0:T(8,128)S(1)} %constant_dynamic-slice_fusion.4, ...), kind=kOutput, calls=%fused_computation.9.clone.1 | convolution fusion | flops 146276352 | bytes 13504517 | tf_op jit(solution)/shard_map/while/body/eval_jaxpr/rhjk,rkhd->rhjd/dot_general | solution.py:134
  271.6 1.0 constant_dynamic-slice_fusion.4
  272.5 3.4 %fusion.62 = (f32[32,2,256]{2,1,0:T(2,128)S(1)}, f32[32,2,128,256]{3,2,1,0:T(8,128)S(1)}) fusion(f32[2,256,128]{1,2,0:T(8,128)S(1)} %constant_dynamic-slice_fusion.4, pred[32,128]{1,0:T(8,128)(4,1)S(1)} %constant_dynamic-slice_fusion.5, bf16[32,256,2,32]{1,3,2,0:T(8,128)(2,1)S(1)} %get-tuple-element.358, ...), kind=kOutput, calls=%fused_computation.3.clone.1 | convolution fusion | flops 140492800 | bytes 10293252 | tf_op jit(solution)/shard_map/while/body/eval_jaxpr/rjhd,rkhd->rhjk/dot_general | solution.py:126
  276.0 3.0 fusion.64
  279.1 3.6 %fusion.66 = f32[32,2,256,32]{2,3,1,0:T(8,128)S(1)} fusion(f32[32,2,256,32]{2,3,1,0:T(8,128)S(1)} %get-tuple-element.342, f32[32,2,128,256]{3,2,1,0:T(8,128)S(1)} %get-tuple-element.323, f32[32,2,256]{2,1,0:T(2,128)S(1)} %fusion.63, f32[2,256,128]{1,2,0:T(8,128)S(1)} %constant_dynamic-slice_fusion.4, ...), kind=kOutput, calls=%fused_computation.9.clone.1 | convolution fusion | flops 146276352 | bytes 13504517 | tf_op jit(solution)/shard_map/while/body/eval_jaxpr/rhjk,rkhd->rhjd/dot_general | solution.py:134
  282.8 1.0 constant_dynamic-slice_fusion.4
  283.8 3.4 %fusion.62 = (f32[32,2,256]{2,1,0:T(2,128)S(1)}, f32[32,2,128,256]{3,2,1,0:T(8,128)S(1)}) fusion(f32[2,256,128]{1,2,0:T(8,128)S(1)} %constant_dynamic-slice_fusion.4, pred[32,128]{1,0:T(8,128)(4,1)S(1)} %constant_dynamic-slice_fusion.5, bf16[32,256,2,32]{1,3,2,0:T(8,128)(2,1)S(1)} %get-tuple-element.358, ...), kind=kOutput, calls=%fused_computation.3.clone.1 | convolution fusion | flops 140492800 | bytes 10293252 | tf_op jit(solution)/shard_map/while/body/eval_jaxpr/rjhd,rkhd->rhjk/dot_general | solution.py:126
  287.2 3.0 fusion.64
  290.4 3.6 %fusion.66 = f32[32,2,256,32]{2,3,1,0:T(8,128)S(1)} fusion(f32[32,2,256,32]{2,3,1,0:T(8,128)S(1)} %get-tuple-element.342, f32[32,2,128,256]{3,2,1,0:T(8,128)S(1)} %get-tuple-element.323, f32[32,2,256]{2,1,0:T(2,128)S(1)} %fusion.63, f32[2,256,128]{1,2,0:T(8,128)S(1)} %constant_dynamic-slice_fusion.4, ...), kind=kOutput, calls=%fused_computation.9.clone.1 | convolution fusion | flops 146276352 | bytes 13504517 | tf_op jit(solution)/shard_map/while/body/eval_jaxpr/rhjk,rkhd->rhjd/dot_general | solution.py:134
  294.4 1.2 copy-done.3
  296.1 1.0 copy.70
  297.0 0.8 reshape.73
  297.9 5.7 %all_to_all.50 = bf16[2,2,65536]{2,1,0:T(2,128)(2,1)S(1)} all-to-all(bf16[2,2,65536]{2,1,0:T(2,128)(2,1)S(1)} %reshape.73), channel_id=1, replica_groups=mesh['groups'=2,'rows'=32,'keys'=4,'heads'=2] {'heads'}, dimensions={0} | all-to-all | bytes 1048576 | tf_op jit(solution)/shard_map/all_to_all | solution.py:52
  303.5 0.7 reshape.74
  304.3 0.9 copy.81
  305.2 1.0 copy.74
  306.2 0.8 reshape.71
  307.1 4.2 %all_to_all.51 = bf16[2,2,65536]{2,1,0:T(2,128)(2,1)S(1)} all-to-all(bf16[2,2,65536]{2,1,0:T(2,128)(2,1)S(1)} %reshape.71), channel_id=1, replica_groups=mesh['groups'=2,'rows'=32,'keys'=4,'heads'=2] {'heads'}, dimensions={0} | all-to-all | bytes 1048576 | tf_op jit(solution)/shard_map/all_to_all | solution.py:52
  311.2 0.7 reshape.72
  312.0 0.9 copy.82
  313.6 1.1 pad_maximum_fusion.1
  (84 shorter events, 6.9 us)
Async XLA Ops:
  6.5 306.4 %copy-start = (bf16[128,128]{1,0:T(8,128)(2,1)S(1)}, bf16[128,128]{1,0:T(8,128)(2,1)}, u32[]{:S(2)}) copy-start(bf16[128,128]{1,0:T(8,128)(2,1)} %param.21) | copy-start | bytes 98308
  6.6 2.4 copy-start.1
  6.6 4.8 %copy-start.9 = (f32[128]{0:T(128)S(1)}, f32[128]{0:T(128)}, u32[]{:S(2)}) copy-start(f32[128]{0:T(128)} %param.15) | copy-start | bytes 1540
  6.6 191.1 %all-gather.2.cloned.1.call-start = ((), (), s32[]{:S(2)}) async-start(), calls=%async_computation.4 | async-start | bytes 10485760 | tf_op jit(solution)/shard_map/all_gather | solution.py:36
  6.6 4.8 %copy-start.2 = (bf16[32,256,128]{2,1,0:T(8,128)(2,1)S(1)}, bf16[32,256,128]{2,1,0:T(8,128)(2,1)}, u32[]{:S(2)}) copy-start(bf16[32,256,128]{2,1,0:T(8,128)(2,1)} %param.12) | copy-start | bytes 6291460
  11.4 2.5 copy-start.5
  14.7 0.9 copy-start.6
  18.8 0.7 copy-start.10
  20.1 48.1 %copy-start.7 = (bf16[128,64]{0,1:T(8,128)(2,1)S(1)}, bf16[128,64]{0,1:T(8,128)(2,1)}, u32[]{:S(2)}) copy-start(bf16[128,64]{0,1:T(8,128)(2,1)} %param.16) | copy-start | bytes 49156
  21.3 150.9 %all-to-all-start = ((bf16[32,2,32,256]{3,2,1,0:T(8,128)(2,1)}), bf16[32,2,32,256]{3,2,1,0:T(8,128)(2,1)}, u32[]{:S(2)}, u32[]{:S(2)}) async-start(bf16[32,2,32,256]{3,2,1,0:T(8,128)(2,1)} %broadcast_in_dim.74), calls=%async_computation | async-start | bytes 2097152 | tf_op jit(solution)/shard_map/all_to_all | solution.py:14
  173.4 6.6 %copy-start.8 = (s32[32,8]{0,1:T(8,128)S(1)}, s32[32,8]{0,1:T(8,128)}, u32[]{:S(2)}) copy-start(s32[32,8]{0,1:T(8,128)} %param.14) | copy-start | bytes 3076
  175.5 18.8 %all-to-all-start.1 = ((bf16[2,1024,256]{2,0,1:T(2,128)(2,1)}), bf16[2,1024,256]{2,0,1:T(2,128)(2,1)}, u32[]{:S(2)}, u32[]{:S(2)}) async-start(bf16[2,1024,256]{2,0,1:T(2,128)(2,1)} %copy.65), calls=%async_computation.1 | async-start | bytes 2097152 | tf_op jit(solution)/shard_map/all_to_all | solution.py:108
  180.1 1.0 copy-start.11
  197.6 6.4 %copy-start.4 = (f32[32,2,256,32]{2,3,1,0:T(8,128)S(1)}, f32[32,2,256,32]{2,3,1,0:T(8,128)}, u32[]{:S(2)}) copy-start(f32[32,2,256,32]{2,3,1,0:T(8,128)} %custom-call.2) | copy-start | bytes 6291460
  294.0 1.6 copy-start.3
Sparse Core Ops, SparseCore 0:
  19.0 126.4 all-gather.1
where the time goes:
time: 323 us; the launch traced here: 322 us
  waiting for transfers between devices  114 us (35%)
  matrix products  62 us (19%)
  starting transfers between devices  50.8 us (16%)
  other arithmetic  36.3 us (11%)
  local copies, waits for them, and re-layouts  33.6 us (10%)
  between operations  14.5 us (4%)
  blocking collectives  9.84 us (3%)
    all_to_all x1, waiting for transfers between devices, from_everyone(): lax.all_to_all(jnp.broadcast_to(value[None], (peers, *value.shape)), axis...  103 us
    all_to_all x1, starting transfers between devices, from_everyone(): lax.all_to_all(jnp.broadcast_to(value[None], (peers, *value.shape)), axis...  46.3 us
    dot_general x8, matrix products, one_tile(): jnp.einsum('rhjk,rkhd->rhjd', weights.astype(jnp.bfloat16), value_tile, p...  28.9 us
    dot_general x8, matrix products, one_tile(): jnp.einsum('rjhd,rkhd->rhjk', queries, key_tile, preferred_element_type=j...  27 us
    reduce_sum x8, other arithmetic, one_tile(): row_sum = row_sum * rescale + jnp.sum(weights, axis=-1)  24 us
    all_to_all x1, waiting for transfers between devices, per_device(): lax.all_to_all(bias_rows.astype(jnp.bfloat16), 'keys', split_axis=1, conc...  10.9 us
    all_to_all x2, blocking collectives, exchange_in_groups(): lax.all_to_all(group, axis, split_axis=split_dim, concat_axis=concat_dim,...  9.84 us
    dynamic_slice x8, local copies, waits for them, and re-layouts, one_tile(): tile_bias = lax.dynamic_slice_in_dim(bias_turn, offset, TILE, 2)  7.84 us
  transfers between devices with their start and end apart: 3, of which 2 were waited for; matrix products, arithmetic and copies ran while one was open for 4% of the time, Pallas kernels for 0%

commit v1 on v0

--- a/solution.py
+++ b/solution.py
@@ -7,6 +7,30 @@
 TILE = 128
 norm_epsilon = 1e-05
 masked_score = -1e30
+
+
+def cut_along(array, dim, size):
+    dims = array.shape
+    pieces = array.reshape(*dims[:dim], size, dims[dim] // size, *dims[dim + 1 :])
+    return jnp.moveaxis(pieces, dim, 0)
+
+
+def in_order(parts, dim):
+    parts = jnp.moveaxis(parts, 0, dim)
+    shape = parts.shape
+    return parts.reshape(*shape[:dim], shape[dim] * shape[dim + 1], *shape[dim + 2 :])
+
+
+def rotated_exchange(x, axis, split_dim, concat_dim):
+    peers, mine = (lax.axis_size(axis), lax.axis_index(axis))
+    tiles = cut_along(x, split_dim, peers)
+    out = tiles
+    for step in range(1, peers):
+        target, source = ((mine + step) % peers, (mine - step) % peers)
+        sent = lax.dynamic_index_in_dim(tiles, target, 0)
+        partner_block = lax.ppermute(sent, axis, [(i, (i + step) % peers) for i in range(peers)])
+        out = lax.dynamic_update_slice_in_dim(out, partner_block, source, axis=0)
+    return in_order(out, concat_dim)
 
 
 def from_everyone(value, axis):
@@ -105,9 +129,9 @@
     allowed = (positions[None, :] < seq_length[0]) & (
         (positions % TILE)[None, :] < jnp.repeat(tile_counts, TILE, axis=1)
     )
-    bias_turn = lax.all_to_all(
-        bias_rows.astype(jnp.bfloat16), "keys", split_axis=1, concat_axis=2, tiled=True
-    ).astype(bias_rows.dtype)
+    bias_turn = rotated_exchange(bias_rows.astype(jnp.bfloat16), "keys", 1, 2).astype(
+        bias_rows.dtype
+    )
     initial = (
         jnp.full((rows_dev, heads_dev, cols_dev), masked_score, jnp.float32),
         jnp.zeros((rows_dev, heads_dev, cols_dev), jnp.float32),

time: 323 us -> 325 us (level)
  waiting for transfers between devices: 114 us -> 104 us
  starting transfers between devices: 50.8 us -> 56.8 us
  local copies, waits for them, and re-layouts: 33.6 us -> 37.3 us
    all_to_all x1 -> x0, waiting for transfers between devices: 10.9 us -> none  [per_device(): lax.all_to_all(bias_rows.astype(jnp.bfloat16), 'keys', split_axis=1, conc...]
    ppermute x0 -> x3, starting transfers between devices: none -> 10.5 us  [rotated_exchange(): lax.ppermute(sent, axis, [(i, (i + step) % peers) for i in range(peers)])]
    dynamic_update_slice x0 -> x3, local copies, waits for them, and re-layouts: none -> 5.01 us  [rotated_exchange(): out = lax.dynamic_update_slice_in_dim(out, partner_block, source, axis=0)]
    all_to_all x1 -> x0, starting transfers between devices: 4.5 us -> none  [per_device(): lax.all_to_all(bias_rows.astype(jnp.bfloat16), 'keys', split_axis=1, conc...]
    ppermute x0 -> x3, waiting for transfers between devices: none -> 3.64 us  [rotated_exchange(): lax.ppermute(sent, axis, [(i, (i + step) % peers) for i in range(peers)])]
  transfers between devices with their start and end apart: 3 -> 5, of which waited for: 2 -> 2; matrix products, arithmetic and copies ran while one was open for 4% -> 5% of each run, Pallas kernels for 0% -> 0%
where the time goes in v1:
time: 325 us; the launch traced here: 323 us
  waiting for transfers between devices  104 us (32%)
  matrix products  62 us (19%)
  starting transfers between devices  56.8 us (17%)
  other arithmetic  37.5 us (12%)
  local copies, waits for them, and re-layouts  37.3 us (11%)
  between operations  14.7 us (5%)
  blocking collectives  10.1 us (3%)
    all_to_all x1, waiting for transfers between devices, from_everyone(): lax.all_to_all(jnp.broadcast_to(value[None], (peers, *value.shape)), axis...  101 us
    all_to_all x1, starting transfers between devices, from_everyone(): lax.all_to_all(jnp.broadcast_to(value[None], (peers, *value.shape)), axis...  46.3 us
    dot_general x8, matrix products, one_tile(): jnp.einsum('rhjk,rkhd->rhjd', weights.astype(jnp.bfloat16), value_tile, p...  28.9 us
    dot_general x8, matrix products, one_tile(): jnp.einsum('rjhd,rkhd->rhjk', queries, key_tile, preferred_element_type=j...  27 us
    reduce_sum x8, other arithmetic, one_tile(): row_sum = row_sum * rescale + jnp.sum(weights, axis=-1)  24 us
    ppermute x3, starting transfers between devices, rotated_exchange(): lax.ppermute(sent, axis, [(i, (i + step) % peers) for i in range(peers)])  10.5 us
    all_to_all x2, blocking collectives, exchange_in_groups(): lax.all_to_all(group, axis, split_axis=split_dim, concat_axis=concat_dim,...  10.1 us
    dynamic_slice x8, local copies, waits for them, and re-layouts, one_tile(): tile_bias = lax.dynamic_slice_in_dim(bias_turn, offset, TILE, 2)  7.84 us
  transfers between devices with their start and end apart: 5, of which 2 were waited for; matrix products, arithmetic and copies ran while one was open for 5% of the time, Pallas kernels for 0%

profile of v1, /device:TPU:33, one launch (start us, length us, event | category | flops | bytes accessed | tf_op | source)
XLA Modules:
  0.0 323.3 jit_solution(5408615050249136512)
XLA Ops:
  6.6 2.4 convert_reduce_fusion
  9.0 2.4 fusion.25
  11.4 2.5 fusion.27
  15.6 0.8 convolution_convert_fusion.1
  17.3 1.6 pad_maximum_fusion
  20.2 1.1 broadcast_in_dim.74
  21.3 46.3 %all-to-all-start = ((bf16[32,2,32,256]{3,2,1,0:T(8,128)(2,1)}), bf16[32,2,32,256]{3,2,1,0:T(8,128)(2,1)}, u32[]{:S(2)}, u32[]{:S(2)}) async-start(bf16[32,2,32,256]{3,2,1,0:T(8,128)(2,1)} %broadcast_in_dim.74), calls=%async_computation | async-start | bytes 2097152 | tf_op jit(solution)/shard_map/all_to_all | solution.py:38
  69.2 2.2 fusion.21
  71.4 100.7 %all-to-all-done = bf16[32,2,32,256]{3,2,1,0:T(8,128)(2,1)} async-done(((bf16[32,2,32,256]{3,2,1,0:T(8,128)(2,1)}), bf16[32,2,32,256]{3,2,1,0:T(8,128)(2,1)}, u32[]{:S(2)}, u32[]{:S(2)}) %all-to-all-start) | async-done | bytes 1048608 | tf_op jit(solution)/shard_map/all_to_all | solution.py:38
  172.1 2.3 copy.62
  174.4 1.2 dynamic-slice_bitcast_fusion
  175.6 3.3 %collective-permute-start = (bf16[1,2,256,256]{3,2,0,1:T(8,128)(2,1)S(1)}, bf16[1,2,256,256]{3,2,0,1:T(8,128)(2,1)}, u32[]{:S(2)}, u32[]{:S(2)}) collective-permute-start(bf16[1,2,256,256]{3,2,0,1:T(8,128)(2,1)S(1)} %get-tuple-element.265), channel_id=1, source_target_pairs={{0,2},{2,4},{4,6},{6,0},{1,3},{3,5},{5,7},{7,1},{8,10},{10,12},{12... | collective-permute-start | bytes 786440 | tf_op jit(solution)/shard_map/ppermute | solution.py:31
  179.0 3.5 %collective-permute-start.2 = (bf16[1,2,256,256]{3,2,0,1:T(8,128)(2,1)S(1)}, bf16[1,2,256,256]{3,2,0,1:T(8,128)(2,1)}, u32[]{:S(2)}, u32[]{:S(2)}) collective-permute-start(bf16[1,2,256,256]{3,2,0,1:T(8,128)(2,1)S(1)} %get-tuple-element.263), channel_id=1, source_target_pairs={{0,6},{2,0},{4,2},{6,4},{1,7},{3,1},{5,3},{7,5},{8,14},{10,8},{12,... | collective-permute-start | bytes 786440 | tf_op jit(solution)/shard_map/ppermute | solution.py:31
  182.4 3.7 %collective-permute-start.1 = (bf16[1,2,256,256]{3,2,0,1:T(8,128)(2,1)S(1)}, bf16[1,2,256,256]{3,2,0,1:T(8,128)(2,1)}, u32[]{:S(2)}, u32[]{:S(2)}) collective-permute-start(bf16[1,2,256,256]{3,2,0,1:T(8,128)(2,1)S(1)} %get-tuple-element.264), channel_id=1, source_target_pairs={{0,4},{2,6},{4,0},{6,2},{1,5},{3,7},{5,1},{7,3},{8,12},{10,14},{12... | collective-permute-start | bytes 786440 | tf_op jit(solution)/shard_map/ppermute | solution.py:31
  187.3 1.7 constant_dynamic-update-slice_fusion.2
  189.0 3.6 %collective-permute-done.1 = bf16[1,2,256,256]{3,2,0,1:T(8,128)(2,1)} collective-permute-done((bf16[1,2,256,256]{3,2,0,1:T(8,128)(2,1)S(1)}, bf16[1,2,256,256]{3,2,0,1:T(8,128)(2,1)}, u32[]{:S(2)}, u32[]{:S(2)}) %collective-permute-start.1) | collective-permute-done | bytes 262176 | tf_op jit(solution)/shard_map/ppermute | solution.py:31
  192.6 1.7 constant_dynamic-update-slice_fusion.1
  194.3 1.7 constant_dynamic-update-slice_fusion
  195.9 1.4 convert_bitcast_fusion
  197.3 1.8 copy.63
  199.2 6.4 %fusion.37 = (bf16[32,1024,2,32]{1,3,2,0:T(8,128)(2,1)}, bf16[32,1024,2,32]{1,3,2,0:T(8,128)(2,1)}) fusion(bf16[64,1024,2,32]{1,3,2,0:T(8,128)(2,1)} %all-gather.2.cloned.1.call-done), kind=kLoop, calls=%fused_computation.69 | loop fusion | bytes 16777216 | tf_op jit(solution)/shard_map/split | solution.py:60
  205.6 90.0 %while.18 = (s32[]{:T(128)}, f32[32,2,256]{2,1,0:T(2,128)S(1)}, f32[32,2,256]{2,1,0:T(2,128)S(1)}, f32[32,2,256,32]{2,3,1,0:T(8,128)S(1)}, pred[32,1024]{1,0:T(8...) while((s32[]{:T(128)}, f32[32,2,256]{2,1,0:T(2,128)S(1)}, ...), condition=%wide.region_5.6_spmd.clone, body=%wide.region_2.5_spmd.clone.sunk | while | flops 297353216 | bytes 33837260 | solution.py:166
  205.6 1.0 constant_dynamic-slice_fusion.4
  206.6 3.4 %fusion.62 = (f32[32,2,256]{2,1,0:T(2,128)S(1)}, f32[32,2,128,256]{3,2,1,0:T(8,128)S(1)}) fusion(f32[2,256,128]{1,2,0:T(8,128)S(1)} %constant_dynamic-slice_fusion.4, pred[32,128]{1,0:T(8,128)(4,1)S(1)} %constant_dynamic-slice_fusion.5, bf16[32,256,2,32]{1,3,2,0:T(8,128)(2,1)S(1)} %get-tuple-element.361, ...), kind=kOutput, calls=%fused_computation.3.clone.1 | convolution fusion | flops 140492800 | bytes 10293252 | tf_op jit(solution)/shard_map/while/body/eval_jaxpr/rjhd,rkhd->rhjk/dot_general | solution.py:150
  210.0 3.0 fusion.64
  213.2 3.6 %fusion.66 = f32[32,2,256,32]{2,3,1,0:T(8,128)S(1)} fusion(f32[32,2,256,32]{2,3,1,0:T(8,128)S(1)} %get-tuple-element.345, f32[32,2,128,256]{3,2,1,0:T(8,128)S(1)} %get-tuple-element.326, f32[32,2,256]{2,1,0:T(2,128)S(1)} %fusion.63, f32[2,256,128]{1,2,0:T(8,128)S(1)} %constant_dynamic-slice_fusion.4, ...), kind=kOutput, calls=%fused_computation.9.clone.1 | convolution fusion | flops 146276352 | bytes 13504517 | tf_op jit(solution)/shard_map/while/body/eval_jaxpr/rhjk,rkhd->rhjd/dot_general | solution.py:158
  216.8 1.0 constant_dynamic-slice_fusion.4
  217.8 3.4 %fusion.62 = (f32[32,2,256]{2,1,0:T(2,128)S(1)}, f32[32,2,128,256]{3,2,1,0:T(8,128)S(1)}) fusion(f32[2,256,128]{1,2,0:T(8,128)S(1)} %constant_dynamic-slice_fusion.4, pred[32,128]{1,0:T(8,128)(4,1)S(1)} %constant_dynamic-slice_fusion.5, bf16[32,256,2,32]{1,3,2,0:T(8,128)(2,1)S(1)} %get-tuple-element.361, ...), kind=kOutput, calls=%fused_computation.3.clone.1 | convolution fusion | flops 140492800 | bytes 10293252 | tf_op jit(solution)/shard_map/while/body/eval_jaxpr/rjhd,rkhd->rhjk/dot_general | solution.py:150
  221.3 3.0 fusion.64
  224.4 3.6 %fusion.66 = f32[32,2,256,32]{2,3,1,0:T(8,128)S(1)} fusion(f32[32,2,256,32]{2,3,1,0:T(8,128)S(1)} %get-tuple-element.345, f32[32,2,128,256]{3,2,1,0:T(8,128)S(1)} %get-tuple-element.326, f32[32,2,256]{2,1,0:T(2,128)S(1)} %fusion.63, f32[2,256,128]{1,2,0:T(8,128)S(1)} %constant_dynamic-slice_fusion.4, ...), kind=kOutput, calls=%fused_computation.9.clone.1 | convolution fusion | flops 146276352 | bytes 13504517 | tf_op jit(solution)/shard_map/while/body/eval_jaxpr/rhjk,rkhd->rhjd/dot_general | solution.py:158
  228.1 1.0 constant_dynamic-slice_fusion.4
  229.1 3.4 %fusion.62 = (f32[32,2,256]{2,1,0:T(2,128)S(1)}, f32[32,2,128,256]{3,2,1,0:T(8,128)S(1)}) fusion(f32[2,256,128]{1,2,0:T(8,128)S(1)} %constant_dynamic-slice_fusion.4, pred[32,128]{1,0:T(8,128)(4,1)S(1)} %constant_dynamic-slice_fusion.5, bf16[32,256,2,32]{1,3,2,0:T(8,128)(2,1)S(1)} %get-tuple-element.361, ...), kind=kOutput, calls=%fused_computation.3.clone.1 | convolution fusion | flops 140492800 | bytes 10293252 | tf_op jit(solution)/shard_map/while/body/eval_jaxpr/rjhd,rkhd->rhjk/dot_general | solution.py:150
  232.5 3.0 fusion.64
  235.7 3.6 %fusion.66 = f32[32,2,256,32]{2,3,1,0:T(8,128)S(1)} fusion(f32[32,2,256,32]{2,3,1,0:T(8,128)S(1)} %get-tuple-element.345, f32[32,2,128,256]{3,2,1,0:T(8,128)S(1)} %get-tuple-element.326, f32[32,2,256]{2,1,0:T(2,128)S(1)} %fusion.63, f32[2,256,128]{1,2,0:T(8,128)S(1)} %constant_dynamic-slice_fusion.4, ...), kind=kOutput, calls=%fused_computation.9.clone.1 | convolution fusion | flops 146276352 | bytes 13504517 | tf_op jit(solution)/shard_map/while/body/eval_jaxpr/rhjk,rkhd->rhjd/dot_general | solution.py:158
  239.3 1.0 constant_dynamic-slice_fusion.4
  240.3 3.4 %fusion.62 = (f32[32,2,256]{2,1,0:T(2,128)S(1)}, f32[32,2,128,256]{3,2,1,0:T(8,128)S(1)}) fusion(f32[2,256,128]{1,2,0:T(8,128)S(1)} %constant_dynamic-slice_fusion.4, pred[32,128]{1,0:T(8,128)(4,1)S(1)} %constant_dynamic-slice_fusion.5, bf16[32,256,2,32]{1,3,2,0:T(8,128)(2,1)S(1)} %get-tuple-element.361, ...), kind=kOutput, calls=%fused_computation.3.clone.1 | convolution fusion | flops 140492800 | bytes 10293252 | tf_op jit(solution)/shard_map/while/body/eval_jaxpr/rjhd,rkhd->rhjk/dot_general | solution.py:150
  243.8 3.0 fusion.64
  246.9 3.6 %fusion.66 = f32[32,2,256,32]{2,3,1,0:T(8,128)S(1)} fusion(f32[32,2,256,32]{2,3,1,0:T(8,128)S(1)} %get-tuple-element.345, f32[32,2,128,256]{3,2,1,0:T(8,128)S(1)} %get-tuple-element.326, f32[32,2,256]{2,1,0:T(2,128)S(1)} %fusion.63, f32[2,256,128]{1,2,0:T(8,128)S(1)} %constant_dynamic-slice_fusion.4, ...), kind=kOutput, calls=%fused_computation.9.clone.1 | convolution fusion | flops 146276352 | bytes 13504517 | tf_op jit(solution)/shard_map/while/body/eval_jaxpr/rhjk,rkhd->rhjd/dot_general | solution.py:158
  250.6 1.0 constant_dynamic-slice_fusion.4
  251.6 3.4 %fusion.62 = (f32[32,2,256]{2,1,0:T(2,128)S(1)}, f32[32,2,128,256]{3,2,1,0:T(8,128)S(1)}) fusion(f32[2,256,128]{1,2,0:T(8,128)S(1)} %constant_dynamic-slice_fusion.4, pred[32,128]{1,0:T(8,128)(4,1)S(1)} %constant_dynamic-slice_fusion.5, bf16[32,256,2,32]{1,3,2,0:T(8,128)(2,1)S(1)} %get-tuple-element.361, ...), kind=kOutput, calls=%fused_computation.3.clone.1 | convolution fusion | flops 140492800 | bytes 10293252 | tf_op jit(solution)/shard_map/while/body/eval_jaxpr/rjhd,rkhd->rhjk/dot_general | solution.py:150
  255.0 3.0 fusion.64
  258.2 3.6 %fusion.66 = f32[32,2,256,32]{2,3,1,0:T(8,128)S(1)} fusion(f32[32,2,256,32]{2,3,1,0:T(8,128)S(1)} %get-tuple-element.345, f32[32,2,128,256]{3,2,1,0:T(8,128)S(1)} %get-tuple-element.326, f32[32,2,256]{2,1,0:T(2,128)S(1)} %fusion.63, f32[2,256,128]{1,2,0:T(8,128)S(1)} %constant_dynamic-slice_fusion.4, ...), kind=kOutput, calls=%fused_computation.9.clone.1 | convolution fusion | flops 146276352 | bytes 13504517 | tf_op jit(solution)/shard_map/while/body/eval_jaxpr/rhjk,rkhd->rhjd/dot_general | solution.py:158
  261.8 1.0 constant_dynamic-slice_fusion.4
  262.8 3.4 %fusion.62 = (f32[32,2,256]{2,1,0:T(2,128)S(1)}, f32[32,2,128,256]{3,2,1,0:T(8,128)S(1)}) fusion(f32[2,256,128]{1,2,0:T(8,128)S(1)} %constant_dynamic-slice_fusion.4, pred[32,128]{1,0:T(8,128)(4,1)S(1)} %constant_dynamic-slice_fusion.5, bf16[32,256,2,32]{1,3,2,0:T(8,128)(2,1)S(1)} %get-tuple-element.361, ...), kind=kOutput, calls=%fused_computation.3.clone.1 | convolution fusion | flops 140492800 | bytes 10293252 | tf_op jit(solution)/shard_map/while/body/eval_jaxpr/rjhd,rkhd->rhjk/dot_general | solution.py:150
  266.3 3.0 fusion.64
  269.4 3.6 %fusion.66 = f32[32,2,256,32]{2,3,1,0:T(8,128)S(1)} fusion(f32[32,2,256,32]{2,3,1,0:T(8,128)S(1)} %get-tuple-element.345, f32[32,2,128,256]{3,2,1,0:T(8,128)S(1)} %get-tuple-element.326, f32[32,2,256]{2,1,0:T(2,128)S(1)} %fusion.63, f32[2,256,128]{1,2,0:T(8,128)S(1)} %constant_dynamic-slice_fusion.4, ...), kind=kOutput, calls=%fused_computation.9.clone.1 | convolution fusion | flops 146276352 | bytes 13504517 | tf_op jit(solution)/shard_map/while/body/eval_jaxpr/rhjk,rkhd->rhjd/dot_general | solution.py:158
  273.1 1.0 constant_dynamic-slice_fusion.4
  274.1 3.4 %fusion.62 = (f32[32,2,256]{2,1,0:T(2,128)S(1)}, f32[32,2,128,256]{3,2,1,0:T(8,128)S(1)}) fusion(f32[2,256,128]{1,2,0:T(8,128)S(1)} %constant_dynamic-slice_fusion.4, pred[32,128]{1,0:T(8,128)(4,1)S(1)} %constant_dynamic-slice_fusion.5, bf16[32,256,2,32]{1,3,2,0:T(8,128)(2,1)S(1)} %get-tuple-element.361, ...), kind=kOutput, calls=%fused_computation.3.clone.1 | convolution fusion | flops 140492800 | bytes 10293252 | tf_op jit(solution)/shard_map/while/body/eval_jaxpr/rjhd,rkhd->rhjk/dot_general | solution.py:150
  277.5 3.0 fusion.64
  280.7 3.6 %fusion.66 = f32[32,2,256,32]{2,3,1,0:T(8,128)S(1)} fusion(f32[32,2,256,32]{2,3,1,0:T(8,128)S(1)} %get-tuple-element.345, f32[32,2,128,256]{3,2,1,0:T(8,128)S(1)} %get-tuple-element.326, f32[32,2,256]{2,1,0:T(2,128)S(1)} %fusion.63, f32[2,256,128]{1,2,0:T(8,128)S(1)} %constant_dynamic-slice_fusion.4, ...), kind=kOutput, calls=%fused_computation.9.clone.1 | convolution fusion | flops 146276352 | bytes 13504517 | tf_op jit(solution)/shard_map/while/body/eval_jaxpr/rhjk,rkhd->rhjd/dot_general | solution.py:158
  284.3 1.0 constant_dynamic-slice_fusion.4
  285.3 3.4 %fusion.62 = (f32[32,2,256]{2,1,0:T(2,128)S(1)}, f32[32,2,128,256]{3,2,1,0:T(8,128)S(1)}) fusion(f32[2,256,128]{1,2,0:T(8,128)S(1)} %constant_dynamic-slice_fusion.4, pred[32,128]{1,0:T(8,128)(4,1)S(1)} %constant_dynamic-slice_fusion.5, bf16[32,256,2,32]{1,3,2,0:T(8,128)(2,1)S(1)} %get-tuple-element.361, ...), kind=kOutput, calls=%fused_computation.3.clone.1 | convolution fusion | flops 140492800 | bytes 10293252 | tf_op jit(solution)/shard_map/while/body/eval_jaxpr/rjhd,rkhd->rhjk/dot_general | solution.py:150
  288.8 3.0 fusion.64
  291.9 3.6 %fusion.66 = f32[32,2,256,32]{2,3,1,0:T(8,128)S(1)} fusion(f32[32,2,256,32]{2,3,1,0:T(8,128)S(1)} %get-tuple-element.345, f32[32,2,128,256]{3,2,1,0:T(8,128)S(1)} %get-tuple-element.326, f32[32,2,256]{2,1,0:T(2,128)S(1)} %fusion.63, f32[2,256,128]{1,2,0:T(8,128)S(1)} %constant_dynamic-slice_fusion.4, ...), kind=kOutput, calls=%fused_computation.9.clone.1 | convolution fusion | flops 146276352 | bytes 13504517 | tf_op jit(solution)/shard_map/while/body/eval_jaxpr/rhjk,rkhd->rhjd/dot_general | solution.py:158
  295.9 1.2 copy-done.3
  297.6 1.0 copy.66
  298.5 0.8 reshape.76
  299.4 5.9 %all_to_all.41 = bf16[2,2,65536]{2,1,0:T(2,128)(2,1)S(1)} all-to-all(bf16[2,2,65536]{2,1,0:T(2,128)(2,1)S(1)} %reshape.76), channel_id=1, replica_groups=mesh['groups'=2,'rows'=32,'keys'=4,'heads'=2] {'heads'}, dimensions={0} | all-to-all | bytes 1048576 | tf_op jit(solution)/shard_map/all_to_all | solution.py:76
  306.0 0.9 copy.77
  307.0 1.0 copy.70
  308.0 0.8 reshape.74
  308.8 4.2 %all_to_all.42 = bf16[2,2,65536]{2,1,0:T(2,128)(2,1)S(1)} all-to-all(bf16[2,2,65536]{2,1,0:T(2,128)(2,1)S(1)} %reshape.74), channel_id=1, replica_groups=mesh['groups'=2,'rows'=32,'keys'=4,'heads'=2] {'heads'}, dimensions={0} | all-to-all | bytes 1048576 | tf_op jit(solution)/shard_map/all_to_all | solution.py:76
  313.7 0.9 copy.78
  315.4 1.1 pad_maximum_fusion.1
  (90 shorter events, 10.5 us)
Async XLA Ops:
  6.5 308.2 %copy-start = (bf16[128,128]{1,0:T(8,128)(2,1)S(1)}, bf16[128,128]{1,0:T(8,128)(2,1)}, u32[]{:S(2)}) copy-start(bf16[128,128]{1,0:T(8,128)(2,1)} %param.21) | copy-start | bytes 98308
  6.6 2.4 copy-start.1
  6.6 4.8 %copy-start.9 = (f32[128]{0:T(128)S(1)}, f32[128]{0:T(128)}, u32[]{:S(2)}) copy-start(f32[128]{0:T(128)} %param.15) | copy-start | bytes 1540
  6.6 192.6 %all-gather.2.cloned.1.call-start = ((), (), s32[]{:S(2)}) async-start(), calls=%async_computation.3 | async-start | bytes 10485760 | tf_op jit(solution)/shard_map/all_gather | solution.py:60
  6.6 4.8 %copy-start.2 = (bf16[32,256,128]{2,1,0:T(8,128)(2,1)S(1)}, bf16[32,256,128]{2,1,0:T(8,128)(2,1)}, u32[]{:S(2)}) copy-start(bf16[32,256,128]{2,1,0:T(8,128)(2,1)} %param.12) | copy-start | bytes 6291460
  11.4 2.5 copy-start.5
  14.7 0.9 copy-start.6
  18.9 0.7 copy-start.10
  20.2 48.2 %copy-start.7 = (bf16[128,64]{0,1:T(8,128)(2,1)S(1)}, bf16[128,64]{0,1:T(8,128)(2,1)}, u32[]{:S(2)}) copy-start(bf16[128,64]{0,1:T(8,128)(2,1)} %param.16) | copy-start | bytes 49156
  21.3 150.9 %all-to-all-start = ((bf16[32,2,32,256]{3,2,1,0:T(8,128)(2,1)}), bf16[32,2,32,256]{3,2,1,0:T(8,128)(2,1)}, u32[]{:S(2)}, u32[]{:S(2)}) async-start(bf16[32,2,32,256]{3,2,1,0:T(8,128)(2,1)} %broadcast_in_dim.74), calls=%async_computation | async-start | bytes 2097152 | tf_op jit(solution)/shard_map/all_to_all | solution.py:38
  68.3 0.9 copy-start.11
  71.4 107.5 %copy-start.8 = (s32[32,8]{0,1:T(8,128)S(1)}, s32[32,8]{0,1:T(8,128)}, u32[]{:S(2)}) copy-start(s32[32,8]{0,1:T(8,128)} %param.14) | copy-start | bytes 3076
  175.6 11.7 %collective-permute-start = (bf16[1,2,256,256]{3,2,0,1:T(8,128)(2,1)S(1)}, bf16[1,2,256,256]{3,2,0,1:T(8,128)(2,1)}, u32[]{:S(2)}, u32[]{:S(2)}) collective-permute-start(bf16[1,2,256,256]{3,2,0,1:T(8,128)(2,1)S(1)} %get-tuple-element.265), channel_id=1, source_target_pairs={{0,2},{2,4},{4,6},{6,0},{1,3},{3,5},{5,7},{7,1},{8,10},{10,12},{12... | collective-permute-start | bytes 786440 | tf_op jit(solution)/shard_map/ppermute | solution.py:31
  179.0 15.3 %collective-permute-start.2 = (bf16[1,2,256,256]{3,2,0,1:T(8,128)(2,1)S(1)}, bf16[1,2,256,256]{3,2,0,1:T(8,128)(2,1)}, u32[]{:S(2)}, u32[]{:S(2)}) collective-permute-start(bf16[1,2,256,256]{3,2,0,1:T(8,128)(2,1)S(1)} %get-tuple-element.263), channel_id=1, source_target_pairs={{0,6},{2,0},{4,2},{6,4},{1,7},{3,1},{5,3},{7,5},{8,14},{10,8},{12,... | collective-permute-start | bytes 786440 | tf_op jit(solution)/shard_map/ppermute | solution.py:31
  182.4 10.1 %collective-permute-start.1 = (bf16[1,2,256,256]{3,2,0,1:T(8,128)(2,1)S(1)}, bf16[1,2,256,256]{3,2,0,1:T(8,128)(2,1)}, u32[]{:S(2)}, u32[]{:S(2)}) collective-permute-start(bf16[1,2,256,256]{3,2,0,1:T(8,128)(2,1)S(1)} %get-tuple-element.264), channel_id=1, source_target_pairs={{0,4},{2,6},{4,0},{6,2},{1,5},{3,7},{5,1},{7,3},{8,12},{10,14},{12... | collective-permute-start | bytes 786440 | tf_op jit(solution)/shard_map/ppermute | solution.py:31
  199.2 6.4 %copy-start.4 = (f32[32,2,256,32]{2,3,1,0:T(8,128)S(1)}, f32[32,2,256,32]{2,3,1,0:T(8,128)}, u32[]{:S(2)}) copy-start(f32[32,2,256,32]{2,3,1,0:T(8,128)} %custom-call.2) | copy-start | bytes 6291460
  295.6 1.6 copy-start.3
Sparse Core Ops, SparseCore 0:
  19.0 126.4 all-gather.1
